TPU v7x, 32 devices: a whole 2x2x4 slice. The times are simulated.
32 devices in a mesh: bank: 4 (over y, x), zero: 8 (over z, core).
Axes of the slice: x: 2, y: 2, z: 4, core: 2. Of those that a mesh axis runs over, the one named last changes fastest.
Arguments:
- train_gate: float32 [64, 2048, 1024], P('bank', 'zero'), may hold values from -0.1875 to 0.1875
- train_up: float32 [64, 2048, 1024], P('bank', 'zero'), may hold values from -0.1875 to 0.1875
- train_down: float32 [64, 1024, 2048], P('bank', None, 'zero'), may hold values from -0.25 to 0.25
- router_weight: float32 [2048, 64], P('zero', 'bank'), may hold values from -0.125 to 0.125
- router_gain: float32 [2048], P('zero'), may hold values from 0.25 to 1.75
Outputs:
- ready_gate: bfloat16 [64, 2048, 1024], P('bank', None, 'zero')
- ready_up: bfloat16 [64, 2048, 1024], P('bank', None, 'zero')
- ready_down: bfloat16 [64, 1024, 2048], P('bank', 'zero')
- scale_gate: float32 [64, 1024], P('bank', 'zero')
- scale_up: float32 [64, 1024], P('bank', 'zero')
- scale_down: float32 [64, 1024], P('bank', 'zero')
- serve_router: bfloat16 [2048, 64], replicated
All inputs are finite; a program needn't handle non-finite values.
Results may differ from a plain program's by a relative error of at most 0.001.
Values may be sent and summed in bfloat16 or wider, within the bound.
A program may use at most 192 MiB of HBM per device.

v0:
```python
import jax
import jax.numpy as jnp
from jax import lax
from jax.sharding import PartitionSpec as P


def on_device(train_gate, train_up, train_down, router_weight, router_gain):
    total_gate, total_up, total_down = lax.psum(
        (
            jnp.sum(train_gate * train_gate, axis=1),
            jnp.sum(train_up * train_up, axis=1),
            jnp.sum(train_down * train_down, axis=2),
        ),
        "zero",
    )
    scale_gate = jnp.sqrt(total_gate)
    scale_up = jnp.sqrt(total_up)
    scale_down = jnp.sqrt(total_down)
    narrow_gate, narrow_up, narrow_down = (
        (train_gate / jnp.expand_dims(scale_gate, 1)).astype(jnp.bfloat16),
        (train_up / jnp.expand_dims(scale_up, 1)).astype(jnp.bfloat16),
        (train_down / jnp.expand_dims(scale_down, 2)).astype(jnp.bfloat16),
    )
    ready_gate, ready_up = (
        lax.all_to_all(narrow_gate, "zero", split_axis=2, concat_axis=1, tiled=True),
        lax.all_to_all(narrow_up, "zero", split_axis=2, concat_axis=1, tiled=True),
    )
    ready_down = lax.all_to_all(narrow_down, "zero", split_axis=1, concat_axis=2, tiled=True)
    scale_gate = lax.dynamic_slice_in_dim(
        scale_gate, lax.axis_index("zero") * ready_gate.shape[2], ready_gate.shape[2], axis=1
    )
    scale_up = lax.dynamic_slice_in_dim(
        scale_up, lax.axis_index("zero") * ready_up.shape[2], ready_up.shape[2], axis=1
    )
    scale_down = lax.dynamic_slice_in_dim(
        scale_down, lax.axis_index("zero") * ready_down.shape[1], ready_down.shape[1], axis=1
    )
    part_router = (router_weight * router_gain[:, None]).astype(jnp.bfloat16)
    row_router = lax.all_gather(part_router, "zero", axis=0, tiled=True)
    serve_router = lax.all_gather(row_router, "bank", axis=1, tiled=True)
    return (ready_gate, ready_up, ready_down, scale_gate, scale_up, scale_down, serve_router)


def solution(mesh):
    return jax.shard_map(
        on_device,
        mesh=mesh,
        in_specs=(
            P("bank", "zero", None),
            P("bank", "zero", None),
            P("bank", None, "zero"),
            P("zero", "bank"),
            P("zero"),
        ),
        out_specs=(
            P("bank", None, "zero"),
            P("bank", None, "zero"),
            P("bank", "zero", None),
            P("bank", "zero"),
            P("bank", "zero"),
            P("bank", "zero"),
            P(),
        ),
        check_vma=False,
    )
```

profile of v0, /device:TPU:0, one launch (start us, length us, event | category | flops | bytes accessed | tf_op | source)
XLA Modules:
  0.0 737.8 jit_solution(13230997140834230480)
XLA Ops:
  7.2 8.6 %multiply_reduce_fusion = f32[16,1024]{1,0:T(8,128)} fusion(f32[16,1024,256]{2,1,0:T(8,128)} %param.7), kind=kLoop, calls=%fused_computation.2 | loop fusion | flops 8372224 | bytes 16842752 | tf_op jit(solution)/shard_map/reduce_sum | solution.py:12
  15.8 12.6 %multiply_reduce_fusion.1 = (f32[16,1024]{1,0:T(8,128)}, f32[16,1024]{1,0:T(8,128)}) fusion(f32[16,256,1024]{2,1,0:T(8,128)} %param.6, f32[16,256,1024]{2,1,0:T(8,128)} %param.5), kind=kLoop, calls=%fused_computation.4 | loop fusion | flops 16744448 | bytes 33685504 | tf_op jit(solution)/shard_map/reduce_sum | solution.py:11
  28.4 17.6 %copy.19 = f32[16,256,1024]{1,0,2:T(8,128)} copy(f32[16,256,1024]{2,1,0:T(8,128)} %param.6) | data formatting | bytes 33554432 | tf_op args[1]
  46.1 40.7 %all-reduce.3.cloned.1.call-done = (f32[16,1024]{1,0:T(8,128)}, f32[16,1024]{1,0:T(8,128)}, f32[16,1024]{1,0:T(8,128)}) async-done(((f32[16,1024]{1,0:T(8,128)}, f32[16,1024]{1,0:T(8,128)}, f32[16,1024]{1,0:T(8,128)}), (f32[16,1024]{1,0:T(8,128)}, f32[16,1024]{1,0:T(8,128)}, f32[16,1024]{1,0:T(8,128)})) %all-reduce.3.cloned.1.call-update) | async-done | bytes 196624 | tf_op jit(solution)/shard_map/psum | solution.py:8
  86.8 0.9 sqrt.10
  87.8 9.6 %divide_convert_fusion = bf16[16,256,1024]{1,0,2:T(8,128)(2,1)} fusion(f32[16,256,1024]{1,0,2:T(8,128)} %copy.19, f32[16,1024]{0,1:T(8,128)S(1)} %copy.18), kind=kLoop, calls=%fused_computation.3 | loop fusion | flops 8388608 | bytes 25231360 | tf_op jit(solution)/shard_map/convert_element_type | solution.py:21
  97.5 4.9 all-to-all-start.1
  102.4 17.6 %copy.16 = f32[16,256,1024]{1,0,2:T(8,128)} copy(f32[16,256,1024]{2,1,0:T(8,128)} %param.5) | data formatting | bytes 33554432 | tf_op args[0]
  120.3 9.7 %divide_convert_fusion.1 = bf16[16,256,1024]{1,0,2:T(8,128)(2,1)} fusion(f32[16,256,1024]{1,0,2:T(8,128)} %copy.16, f32[16,1024]{0,1:T(8,128)S(1)} %copy.15), kind=kLoop, calls=%fused_computation.5 | loop fusion | flops 8388608 | bytes 25231360 | tf_op jit(solution)/shard_map/convert_element_type | solution.py:20
  130.0 156.3 %all-to-all-done.1 = bf16[16,256,1024]{1,0,2:T(8,128)(2,1)} async-done(((bf16[16,256,1024]{1,0,2:T(8,128)(2,1)}), bf16[16,256,1024]{1,0,2:T(8,128)(2,1)}, u32[]{:S(2)}, u32[]{:S(2)}) %all-to-all-start.1) | async-done | bytes 8388640 | tf_op jit(solution)/shard_map/all_to_all | solution.py:26
  286.3 4.9 all-to-all-start
  291.5 16.6 %fusion = bf16[16,1024,256]{2,0,1:T(8,128)(2,1)} fusion(f32[16,1024,256]{2,1,0:T(8,128)} %param.7, f32[16,1024]{0,1:T(8,128)S(1)} %copy.21), kind=kLoop, calls=%fused_computation.1 | loop fusion | flops 8388608 | bytes 25231360 | tf_op jit(solution)/shard_map/convert_element_type | solution.py:22
  308.1 167.0 %all-to-all-done = bf16[16,256,1024]{1,0,2:T(8,128)(2,1)} async-done(((bf16[16,256,1024]{1,0,2:T(8,128)(2,1)}), bf16[16,256,1024]{1,0,2:T(8,128)(2,1)}, u32[]{:S(2)}, u32[]{:S(2)}) %all-to-all-start) | async-done | bytes 8388640 | tf_op jit(solution)/shard_map/all_to_all | solution.py:25
  475.1 5.0 all-to-all-start.2
  480.2 189.9 %all_gather.6 = bf16[2048,16]{0,1:T(8,128)(2,1)S(1)} all-gather(bf16[256,16]{0,1:T(8,128)(2,1)S(1)} %multiply_convert_fusion), channel_id=1, replica_groups=mesh['bank'=4,'zero'=8] {'zero'}, dimensions={0}, use_global_device_ids=true | all-gather | bytes 73728 | tf_op jit(solution)/shard_map/all_gather | solution.py:39
  670.0 9.1 %all_gather.7 = bf16[2048,64]{0,1:T(8,128)(2,1)S(1)} all-gather(bf16[2048,16]{0,1:T(8,128)(2,1)S(1)} %all_gather.6), channel_id=1, replica_groups=mesh['bank'=4,'zero'=8] {'bank'}, dimensions={1}, use_global_device_ids=true | all-gather | bytes 327680 | tf_op jit(solution)/shard_map/all_gather | solution.py:40
  679.1 0.6 constant_dynamic-slice_fusion
  679.7 0.6 constant_dynamic-slice_fusion.1
  680.3 0.6 constant_dynamic-slice_fusion.2
  680.9 12.3 %copy.20 = bf16[16,8,256,128]{3,2,1,0:T(8,128)(2,1)} copy(bf16[16,8,256,128]{2,0,3,1:T(8,128)(2,1)} %bitcast.4) | data formatting | bytes 16777216 | tf_op jit(solution)/shard_map/all_to_all | solution.py:26
  693.2 12.3 %copy.17 = bf16[16,8,256,128]{3,2,1,0:T(8,128)(2,1)} copy(bf16[16,8,256,128]{2,0,3,1:T(8,128)(2,1)} %bitcast.1) | data formatting | bytes 16777216 | tf_op jit(solution)/shard_map/all_to_all | solution.py:25
  705.5 11.4 %copy.23 = bf16[16,128,8,256]{3,2,1,0:T(8,128)(2,1)} copy(bf16[16,128,8,256]{3,0,1,2:T(8,128)(2,1)} %bitcast.7) | data formatting | bytes 16777216 | tf_op jit(solution)/shard_map/all_to_all | solution.py:28
  716.9 13.4 %all_to_all.50 = bf16[16,128,2048]{2,1,0:T(8,128)(2,1)} reshape(bf16[16,128,8,256]{3,2,1,0:T(8,128)(2,1)} %copy.23) | data formatting | bytes 16777216 | tf_op jit(solution)/shard_map/all_to_all | solution.py:28
  730.3 0.7 copy.31
  (17 shorter events, 0.7 us)
Async XLA Ops:
  7.2 79.6 %all-reduce.3.cloned.1.call-start = ((), (), s32[]{:S(2)}) async-start(), calls=%async_computation.3 | async-start | bytes 393216 | tf_op jit(solution)/shard_map/psum | solution.py:8
  97.5 188.8 %all-to-all-start.1 = ((bf16[16,256,1024]{1,0,2:T(8,128)(2,1)}), bf16[16,256,1024]{1,0,2:T(8,128)(2,1)}, u32[]{:S(2)}, u32[]{:S(2)}) async-start(bf16[16,256,1024]{1,0,2:T(8,128)(2,1)} %divide_convert_fusion), calls=%async_computation.1 | async-start | bytes 16777216 | tf_op jit(solution)/shard_map/all_to_all | solution.py:26
  102.4 17.6 %copy-start.1 = (f32[16,1024]{1,0:T(8,128)S(1)}, f32[16,1024]{1,0:T(8,128)}, u32[]{:S(2)}) copy-start(f32[16,1024]{1,0:T(8,128)} %get-tuple-element.7) | copy-start | bytes 196612
  120.3 170.9 %copy-start = (f32[16,1024]{1,0:T(8,128)S(1)}, f32[16,1024]{1,0:T(8,128)}, u32[]{:S(2)}) copy-start(f32[16,1024]{1,0:T(8,128)} %get-tuple-element.9) | copy-start | bytes 196612
  286.3 188.8 %all-to-all-start = ((bf16[16,256,1024]{1,0,2:T(8,128)(2,1)}), bf16[16,256,1024]{1,0,2:T(8,128)(2,1)}, u32[]{:S(2)}, u32[]{:S(2)}) async-start(bf16[16,256,1024]{1,0,2:T(8,128)(2,1)} %divide_convert_fusion.1), calls=%async_computation | async-start | bytes 16777216 | tf_op jit(solution)/shard_map/all_to_all | solution.py:25
  291.5 188.6 %copy-start.2 = (f32[256,16]{0,1:T(8,128)S(1)}, f32[256,16]{0,1:T(8,128)}, u32[]{:S(2)}) copy-start(f32[256,16]{0,1:T(8,128)} %param.8) | copy-start | bytes 49156
  291.5 188.6 %copy-start.3 = (f32[256]{0:T(256)S(1)}, f32[256]{0:T(256)}, u32[]{:S(2)}) copy-start(f32[256]{0:T(256)} %param.9) | copy-start | bytes 3076
  475.1 230.4 %all-to-all-start.2 = ((bf16[16,1024,256]{2,0,1:T(8,128)(2,1)}), bf16[16,1024,256]{2,0,1:T(8,128)(2,1)}, u32[]{:S(2)}, u32[]{:S(2)}) async-start(bf16[16,1024,256]{2,0,1:T(8,128)(2,1)} %fusion), calls=%async_computation.2 | async-start | bytes 16777216 | tf_op jit(solution)/shard_map/all_to_all | solution.py:28
Sparse Core Ops, SparseCore 0:
  28.6 58.1 all-reduce.2
where the time goes:
time: 740 us; the launch traced here: 738 us
  waiting for transfers between devices  364 us (49%)
  blocking collectives  199 us (27%)
  local copies, waits for them, and re-layouts  88.6 us (12%)
  other arithmetic  57.2 us (8%)
  starting transfers between devices  14.9 us (2%)
  between operations  14.2 us (2%)
    all_gather x1, blocking collectives, on_device(): row_router = lax.all_gather(part_router, 'zero', axis=0, tiled=True)  190 us
    all_to_all x1, waiting for transfers between devices, on_device(): lax.all_to_all(narrow_gate, 'zero', split_axis=2, concat_axis=1, tiled=True)  167 us
    all_to_all x1, waiting for transfers between devices, on_device(): lax.all_to_all(narrow_up, 'zero', split_axis=2, concat_axis=1, tiled=True)  156 us
    psum x1, waiting for transfers between devices, on_device(): lax.psum((jnp.sum(train_gate * train_gate, axis=1), jnp.sum(train_up * tr...  40.7 us
    unnamed x11, local copies, waits for them, and re-layouts  36 us
    all_to_all x2, local copies, waits for them, and re-layouts, on_device(): lax.all_to_all(narrow_down, 'zero', split_axis=1, concat_axis=2, tiled=True)  24.8 us
    convert_element_type x1, other arithmetic, on_device(): (train_down / jnp.expand_dims(scale_down, 2)).astype(jnp.bfloat16)  16.6 us
  transfers between devices with their start and end apart: 4, of which 3 were waited for; matrix products, arithmetic and copies ran while one was open for 12% of the time, Pallas kernels for 0%

commit v1 on v0

--- a/solution.py
+++ b/solution.py
@@ -37,7 +37,9 @@
     )
     part_router = (router_weight * router_gain[:, None]).astype(jnp.bfloat16)
     row_router = lax.all_gather(part_router, "zero", axis=0, tiled=True)
-    serve_router = lax.all_gather(row_router, "bank", axis=1, tiled=True)
+    serve_router = jnp.concatenate(
+        lax.all_to_all(jnp.stack([row_router] * lax.axis_size("bank")), "bank", 0, 0), axis=1
+    )
     return (ready_gate, ready_up, ready_down, scale_gate, scale_up, scale_down, serve_router)
 
 

time: 740 us -> 698 us (0.943)
  blocking collectives: 199 us -> 15.7 us
  waiting for transfers between devices: 364 us -> 501 us
    all_gather x1, blocking collectives: 190 us -> 15.7 us  [on_device(): row_router = lax.all_gather(part_router, 'zero', axis=0, tiled=True)]
    all_to_all x1, waiting for transfers between devices: 0.01 us -> 157 us  [on_device(): lax.all_to_all(narrow_down, 'zero', split_axis=1, concat_axis=2, tiled=True)]
    psum x1, waiting for transfers between devices: 40.7 us -> 20.6 us  [on_device(): lax.psum((jnp.sum(train_gate * train_gate, axis=1), jnp.sum(train_up * tr...]
    all_gather x1 -> x0, blocking collectives: 9.11 us -> none  [on_device(): serve_router = lax.all_gather(row_router, 'bank', axis=1, tiled=True)]
  transfers between devices with their start and end apart: 4 -> 5, of which waited for: 3 -> 4; matrix products, arithmetic and copies ran while one was open for 12% -> 14% of each run, Pallas kernels for 0% -> 0%
where the time goes in v1:
time: 698 us; the launch traced here: 696 us
  waiting for transfers between devices  501 us (72%)
  local copies, waits for them, and re-layouts  89.3 us (13%)
  other arithmetic  57.2 us (8%)
  starting transfers between devices  18.9 us (3%)
  blocking collectives  15.7 us (2%)
  between operations  14.2 us (2%)
    all_to_all x1, waiting for transfers between devices, on_device(): lax.all_to_all(narrow_gate, 'zero', split_axis=2, concat_axis=1, tiled=True)  167 us
    all_to_all x1, waiting for transfers between devices, on_device(): lax.all_to_all(narrow_down, 'zero', split_axis=1, concat_axis=2, tiled=True)  157 us
    all_to_all x1, waiting for transfers between devices, on_device(): lax.all_to_all(narrow_up, 'zero', split_axis=2, concat_axis=1, tiled=True)  156 us
    unnamed x11, local copies, waits for them, and re-layouts  35.9 us
    all_to_all x2, local copies, waits for them, and re-layouts, on_device(): lax.all_to_all(narrow_down, 'zero', split_axis=1, concat_axis=2, tiled=True)  24.8 us
    psum x1, waiting for transfers between devices, on_device(): lax.psum((jnp.sum(train_gate * train_gate, axis=1), jnp.sum(train_up * tr...  20.6 us
    convert_element_type x1, other arithmetic, on_device(): (train_down / jnp.expand_dims(scale_down, 2)).astype(jnp.bfloat16)  16.6 us
    all_gather x1, blocking collectives, on_device(): row_router = lax.all_gather(part_router, 'zero', axis=0, tiled=True)  15.7 us
  transfers between devices with their start and end apart: 5, of which 4 were waited for; matrix products, arithmetic and copies ran while one was open for 14% of the time, Pallas kernels for 0%

profile of v1, /device:TPU:0, one launch (start us, length us, event | category | flops | bytes accessed | tf_op | source)
XLA Modules:
  0.0 696.4 jit_solution(11741633743572028333)
XLA Ops:
  7.2 8.6 %multiply_reduce_fusion = f32[16,1024]{1,0:T(8,128)} fusion(f32[16,1024,256]{2,1,0:T(8,128)} %param.7), kind=kLoop, calls=%fused_computation.2 | loop fusion | flops 8372224 | bytes 16842752 | tf_op jit(solution)/shard_map/reduce_sum | solution.py:12
  15.9 12.6 %multiply_reduce_fusion.1 = (f32[16,1024]{1,0:T(8,128)}, f32[16,1024]{1,0:T(8,128)}) fusion(f32[16,256,1024]{2,1,0:T(8,128)} %param.6, f32[16,256,1024]{2,1,0:T(8,128)} %param.5), kind=kLoop, calls=%fused_computation.4 | loop fusion | flops 16744448 | bytes 33685504 | tf_op jit(solution)/shard_map/reduce_sum | solution.py:11
  28.5 15.7 %all_gather.3 = bf16[2048,16]{0,1:T(8,128)(2,1)S(1)} all-gather(bf16[256,16]{0,1:T(8,128)(2,1)S(1)} %multiply_convert_fusion), channel_id=1, replica_groups=mesh['bank'=4,'zero'=8] {'zero'}, dimensions={0}, use_global_device_ids=true | all-gather | bytes 73728 | tf_op jit(solution)/shard_map/all_gather | solution.py:39
  44.2 0.7 stack.2
  44.9 3.7 all-to-all-start.3
  48.6 17.6 %copy.19 = f32[16,256,1024]{1,0,2:T(8,128)} copy(f32[16,256,1024]{2,1,0:T(8,128)} %param.6) | data formatting | bytes 33554432 | tf_op args[1]
  66.2 20.6 %all-reduce.3.cloned.1.call-done = (f32[16,1024]{1,0:T(8,128)}, f32[16,1024]{1,0:T(8,128)}, f32[16,1024]{1,0:T(8,128)}) async-done(((f32[16,1024]{1,0:T(8,128)}, f32[16,1024]{1,0:T(8,128)}, f32[16,1024]{1,0:T(8,128)}), (f32[16,1024]{1,0:T(8,128)}, f32[16,1024]{1,0:T(8,128)}, f32[16,1024]{1,0:T(8,128)})) %all-reduce.3.cloned.1.call-update) | async-done | bytes 196624 | tf_op jit(solution)/shard_map/psum | solution.py:8
  86.8 0.9 sqrt.10
  87.8 9.6 %divide_convert_fusion = bf16[16,256,1024]{1,0,2:T(8,128)(2,1)} fusion(f32[16,256,1024]{1,0,2:T(8,128)} %copy.19, f32[16,1024]{0,1:T(8,128)S(1)} %copy.18), kind=kLoop, calls=%fused_computation.3 | loop fusion | flops 8388608 | bytes 25231360 | tf_op jit(solution)/shard_map/convert_element_type | solution.py:21
  97.5 5.0 all-to-all-start.1
  102.5 17.6 %copy.16 = f32[16,256,1024]{1,0,2:T(8,128)} copy(f32[16,256,1024]{2,1,0:T(8,128)} %param.5) | data formatting | bytes 33554432 | tf_op args[0]
  120.3 9.7 %divide_convert_fusion.1 = bf16[16,256,1024]{1,0,2:T(8,128)(2,1)} fusion(f32[16,256,1024]{1,0,2:T(8,128)} %copy.16, f32[16,1024]{0,1:T(8,128)S(1)} %copy.15), kind=kLoop, calls=%fused_computation.5 | loop fusion | flops 8388608 | bytes 25231360 | tf_op jit(solution)/shard_map/convert_element_type | solution.py:20
  130.0 156.3 %all-to-all-done.1 = bf16[16,256,1024]{1,0,2:T(8,128)(2,1)} async-done(((bf16[16,256,1024]{1,0,2:T(8,128)(2,1)}), bf16[16,256,1024]{1,0,2:T(8,128)(2,1)}, u32[]{:S(2)}, u32[]{:S(2)}) %all-to-all-start.1) | async-done | bytes 8388640 | tf_op jit(solution)/shard_map/all_to_all | solution.py:26
  286.3 4.9 all-to-all-start
  291.5 16.6 %fusion = bf16[16,1024,256]{2,0,1:T(8,128)(2,1)} fusion(f32[16,1024,256]{2,1,0:T(8,128)} %param.7, f32[16,1024]{0,1:T(8,128)S(1)} %copy.21), kind=kLoop, calls=%fused_computation.1 | loop fusion | flops 8388608 | bytes 25231360 | tf_op jit(solution)/shard_map/convert_element_type | solution.py:22
  308.1 167.0 %all-to-all-done = bf16[16,256,1024]{1,0,2:T(8,128)(2,1)} async-done(((bf16[16,256,1024]{1,0,2:T(8,128)(2,1)}), bf16[16,256,1024]{1,0,2:T(8,128)(2,1)}, u32[]{:S(2)}, u32[]{:S(2)}) %all-to-all-start) | async-done | bytes 8388640 | tf_op jit(solution)/shard_map/all_to_all | solution.py:25
  475.1 5.2 all-to-all-start.2
  480.3 0.6 constant_dynamic-slice_fusion
  482.2 12.3 %copy.20 = bf16[16,8,256,128]{3,2,1,0:T(8,128)(2,1)} copy(bf16[16,8,256,128]{2,0,3,1:T(8,128)(2,1)} %bitcast.4) | data formatting | bytes 16777216 | tf_op jit(solution)/shard_map/all_to_all | solution.py:26
  494.4 12.3 %copy.17 = bf16[16,8,256,128]{3,2,1,0:T(8,128)(2,1)} copy(bf16[16,8,256,128]{2,0,3,1:T(8,128)(2,1)} %bitcast.1) | data formatting | bytes 16777216 | tf_op jit(solution)/shard_map/all_to_all | solution.py:25
  506.7 157.3 %all-to-all-done.2 = bf16[16,1024,256]{2,0,1:T(8,128)(2,1)} async-done(((bf16[16,1024,256]{2,0,1:T(8,128)(2,1)}), bf16[16,1024,256]{2,0,1:T(8,128)(2,1)}, u32[]{:S(2)}, u32[]{:S(2)}) %all-to-all-start.2) | async-done | bytes 8388640 | tf_op jit(solution)/shard_map/all_to_all | solution.py:28
  664.0 11.4 %copy.23 = bf16[16,128,8,256]{3,2,1,0:T(8,128)(2,1)} copy(bf16[16,128,8,256]{3,0,1,2:T(8,128)(2,1)} %bitcast.7) | data formatting | bytes 16777216 | tf_op jit(solution)/shard_map/all_to_all | solution.py:28
  675.4 13.4 %all_to_all.53 = bf16[16,128,2048]{2,1,0:T(8,128)(2,1)} reshape(bf16[16,128,8,256]{3,2,1,0:T(8,128)(2,1)} %copy.23) | data formatting | bytes 16777216 | tf_op jit(solution)/shard_map/all_to_all | solution.py:28
  688.8 0.7 copy.31
  (19 shorter events, 1.9 us)
Async XLA Ops:
  7.2 79.6 %all-reduce.3.cloned.1.call-start = ((), (), s32[]{:S(2)}) async-start(), calls=%async_computation.4 | async-start | bytes 393216 | tf_op jit(solution)/shard_map/psum | solution.py:8
  15.8 12.6 %copy-start.2 = (f32[256,16]{0,1:T(8,128)S(1)}, f32[256,16]{0,1:T(8,128)}, u32[]{:S(2)}) copy-start(f32[256,16]{0,1:T(8,128)} %param.8) | copy-start | bytes 49156
  15.8 12.6 %copy-start.3 = (f32[256]{0:T(256)S(1)}, f32[256]{0:T(256)}, u32[]{:S(2)}) copy-start(f32[256]{0:T(256)} %param.9) | copy-start | bytes 3076
  44.9 52.6 %all-to-all-start.3 = ((bf16[4,2048,16]{1,2,0:T(8,128)(2,1)}), bf16[4,2048,16]{1,2,0:T(8,128)(2,1)S(1)}, u32[]{:S(2)}, u32[]{:S(2)}) async-start(bf16[4,2048,16]{1,2,0:T(8,128)(2,1)} %stack.2), calls=%async_computation.3 | async-start | bytes 524288 | tf_op jit(solution)/shard_map/all_to_all | solution.py:41
  97.5 188.8 %all-to-all-start.1 = ((bf16[16,256,1024]{1,0,2:T(8,128)(2,1)}), bf16[16,256,1024]{1,0,2:T(8,128)(2,1)}, u32[]{:S(2)}, u32[]{:S(2)}) async-start(bf16[16,256,1024]{1,0,2:T(8,128)(2,1)} %divide_convert_fusion), calls=%async_computation.1 | async-start | bytes 16777216 | tf_op jit(solution)/shard_map/all_to_all | solution.py:26
  102.5 17.6 %copy-start.1 = (f32[16,1024]{1,0:T(8,128)S(1)}, f32[16,1024]{1,0:T(8,128)}, u32[]{:S(2)}) copy-start(f32[16,1024]{1,0:T(8,128)} %get-tuple-element.7) | copy-start | bytes 196612
  120.3 171.0 %copy-start = (f32[16,1024]{1,0:T(8,128)S(1)}, f32[16,1024]{1,0:T(8,128)}, u32[]{:S(2)}) copy-start(f32[16,1024]{1,0:T(8,128)} %get-tuple-element.9) | copy-start | bytes 196612
  286.3 188.8 %all-to-all-start = ((bf16[16,256,1024]{1,0,2:T(8,128)(2,1)}), bf16[16,256,1024]{1,0,2:T(8,128)(2,1)}, u32[]{:S(2)}, u32[]{:S(2)}) async-start(bf16[16,256,1024]{1,0,2:T(8,128)(2,1)} %divide_convert_fusion.1), calls=%async_computation | async-start | bytes 16777216 | tf_op jit(solution)/shard_map/all_to_all | solution.py:25
  475.1 188.9 %all-to-all-start.2 = ((bf16[16,1024,256]{2,0,1:T(8,128)(2,1)}), bf16[16,1024,256]{2,0,1:T(8,128)(2,1)}, u32[]{:S(2)}, u32[]{:S(2)}) async-start(bf16[16,1024,256]{2,0,1:T(8,128)(2,1)} %fusion), calls=%async_computation.2 | async-start | bytes 16777216 | tf_op jit(solution)/shard_map/all_to_all | solution.py:28
Sparse Core Ops, SparseCore 0:
  28.6 58.1 all-reduce.2
